TPU v7x, 512 devices: a whole 4x8x8 slice. The times are simulated.
512 devices in a mesh: hx: 4 (over y_hi), hy: 4 (over x), tok: 32 (over y_lo, z, core).
Axes of the slice: x: 4, y: 8 (y_hi: 4, y_lo: 2; y = y_hi * 2 + y_lo), z: 8, core: 2. Of those that a mesh axis runs over, the one named last changes fastest.
Arguments:
- stream_in: bfloat16 [8192, 4608], P('tok', ('hx', 'hy')), may hold values from -6 to 6
- before_gain: bfloat16 [4608], P(('hx', 'hy')), may hold values from 0.25 to 1.75
- after_gain: bfloat16 [4608], P(('hx', 'hy')), may hold values from 0.25 to 1.75
- feed_gain: bfloat16 [4608], P(('hx', 'hy')), may hold values from 0.25 to 1.75
- query_weight: bfloat16 [4608, 4096], P('tok', ('hx', 'hy')), may hold values from -1 to 1
- key_weight: bfloat16 [4608, 2048], P('tok', ('hx', 'hy')), may hold values from -64 to 64
- value_weight: bfloat16 [4608, 2048], P('tok', ('hx', 'hy')), may hold values from -0.09375 to 0.09375
- output_weight: bfloat16 [4096, 4608], P(('hx', 'hy'), 'tok'), may hold values from -0.09375 to 0.09375
- documents: int32 [8192], P('tok'), may hold values from 0 to 127, never falling along the last dimension, each value on 1 to 128 neighbouring positions
Outputs:
- residual: bfloat16 [8192, 4608], P('tok', ('hx', 'hy'))
- feed_input: bfloat16 [8192, 4608], P('tok', ('hx', 'hy'))
Inputs may be any that keep to these rules, and one draw needn't show every extreme that they name: `documents`: ids never fall along the tokens; a document holds at most 128 tokens and may run across a sequence's end.
All inputs are finite; a program needn't handle non-finite values.
Results may differ from a plain program's by a relative error of at most 0.014.
The roundings to bfloat16 on the way count: a program that leaves them out, or rounds other values in their place, can miss the bound.
Values may be sent and summed in bfloat16 or wider, within the bound.
No kernel may reach another device: no remote copies, remote signals or barrier semaphores. Data moves between devices by JAX's collectives and lax.ppermute only.
A program may use at most 64 MiB of HBM per device.

v0:
```python
import jax
import jax.numpy as jnp
from jax import lax
from jax.sharding import PartitionSpec as P

D = 4608
QH = 32
HEAD = 128
LENGTH = 256
epsilon = 1e-06
neg_big = -1e30


def rows_first(arrays, axis, dims):
    turned = [jnp.moveaxis(a, dim, 0) for a, dim in zip(arrays, dims)]
    both = jnp.concatenate([t.reshape(len(t), -1) for t in turned], axis=1)
    filled, at, finished = (lax.all_gather(both, axis, axis=0, tiled=True), 0, [])
    for t, dim in zip(turned, dims):
        slab = filled[:, at : at + t[0].size].reshape(-1, *t.shape[1:])
        finished.append(jnp.moveaxis(slab, 0, dim))
        at += t[0].size
    return tuple(finished)


def side_by_side(arrays, axis, dim, along):
    widths = [a.shape[along] for a in arrays]
    both = jnp.concatenate(arrays, axis=along)
    filled = lax.all_gather(both, axis, axis=dim, tiled=True)
    return tuple(jnp.split(filled, [sum(widths[:k]) for k in range(1, len(widths))], axis=along))


def copy_for_each(value, axis):
    copies = jnp.broadcast_to(value, (lax.axis_size(axis), *value.shape))
    return lax.all_to_all(copies, axis, split_axis=0, concat_axis=0, tiled=True)


def joined_along(parts, dim):
    dims = list(parts.shape[1:])
    dims[dim] *= parts.shape[0]
    return jnp.moveaxis(parts, 0, dim).reshape(dims)


def gathered_copies(value, axis, dim):
    parts = copy_for_each(value, axis)
    return joined_along(parts, dim)


def over_copies(value, axis):
    return copy_for_each(value, axis).sum(axis=0)


def in_one(arrays, axis):
    ravelled, at, finished = (jnp.concatenate([a.reshape(-1) for a in arrays]), 0, [])
    subtotal = over_copies(ravelled, axis)
    for a in arrays:
        finished.append(subtotal[at : at + a.size].reshape(a.shape))
        at += a.size
    return tuple(finished)


def rotate(values, positions):
    half_width = values.shape[-1] // 2
    frequency = 10000.0 ** (-jnp.arange(half_width, dtype=jnp.float32) / half_width)
    angles = positions.astype(jnp.float32)[:, None] * frequency[None, :]
    cosine_table = jnp.cos(angles)[:, None, :]
    sine_table = jnp.sin(angles)[:, None, :]
    leading = values[..., :half_width]
    trailing = values[..., half_width:]
    return jnp.concatenate(
        [
            leading * cosine_table - trailing * sine_table,
            trailing * cosine_table + leading * sine_table,
        ],
        axis=-1,
    )


def per_device(
    stream_in,
    before_gain,
    after_gain,
    feed_gain,
    query_weight,
    key_weight,
    value_weight,
    output_weight,
    documents,
):
    rows = stream_in.shape[0]
    wide = stream_in.astype(jnp.float32)
    raw_rows, gain_whole = rows_first((stream_in, before_gain), ("hx", "hy"), (1, 0))
    raw_wide = raw_rows.astype(jnp.float32)
    first_sq = jnp.sum(raw_wide * raw_wide, axis=1)
    first_scale = lax.rsqrt(first_sq / D + epsilon)
    normed = (raw_wide * first_scale[:, None] * gain_whole.astype(jnp.float32)[None, :]).astype(
        jnp.bfloat16
    )
    pieces = side_by_side((query_weight, key_weight, value_weight), "tok", 0, 1)
    query_sum, key_sum, value_sum = tuple(
        (jnp.dot(normed, piece, preferred_element_type=jnp.float32) for piece in pieces)
    )
    query_heads = query_weight.shape[1] // HEAD
    key_heads = key_weight.shape[1] // HEAD
    ratio = query_heads // key_heads
    positions = jnp.arange(rows, dtype=jnp.int32) % LENGTH
    count_seq = rows // LENGTH
    queries = (
        (rotate(query_sum.reshape(rows, query_heads, HEAD), positions) * (D / QH) ** (-0.5))
        .astype(jnp.bfloat16)
        .reshape(count_seq, LENGTH, key_heads, ratio, HEAD)
    )
    keys = (
        rotate(key_sum.reshape(rows, key_heads, HEAD), positions)
        .astype(jnp.bfloat16)
        .reshape(count_seq, LENGTH, key_heads, HEAD)
    )
    values = value_sum.astype(jnp.bfloat16).reshape(count_seq, LENGTH, key_heads, HEAD)
    doc_seq = documents.reshape(count_seq, LENGTH)

    def one_sequence(items):
        query_part, key_part, value_part, doc_part = items
        scores = jnp.einsum(
            "tkrh,skh->tkrs", query_part, key_part, preferred_element_type=jnp.float32
        )
        index = jnp.arange(LENGTH)
        allowed = (index[None, :] <= index[:, None]) & (doc_part[None, :] == doc_part[:, None])
        mask = allowed[:, None, None, :]
        best = jnp.max(jnp.where(mask, scores, neg_big), axis=-1, keepdims=True)
        weights = jnp.where(mask, jnp.exp(scores - best), 0.0)
        total = jnp.sum(weights, axis=-1)
        summed = jnp.einsum(
            "tkrs,skh->tkrh",
            weights.astype(jnp.bfloat16),
            value_part,
            preferred_element_type=jnp.float32,
        )
        return (summed / total[..., None]).astype(jnp.bfloat16)

    attended = lax.map(one_sequence, (queries, keys, values, doc_seq)).reshape(
        rows, query_heads * HEAD
    )
    terms = jnp.dot(
        attended, gathered_copies(output_weight, "tok", 1), preferred_element_type=jnp.float32
    )
    mixed = lax.psum_scatter(
        terms.astype(jnp.bfloat16), ("hx", "hy"), scatter_dimension=1, tiled=True
    ).astype(jnp.float32)
    gain_after = after_gain.astype(jnp.float32)[None, :]
    gain_feed = feed_gain.astype(jnp.float32)[None, :]
    branch = mixed * gain_after
    after_sq, cross_sum, branch_sq = in_one(
        (
            jnp.sum(mixed * mixed, axis=1),
            jnp.sum(wide * branch, axis=1),
            jnp.sum(branch * branch, axis=1),
        ),
        ("hx", "hy"),
    )
    after_scale = lax.rsqrt(after_sq / D + epsilon)
    residual = (wide + mixed * after_scale[:, None] * gain_after).astype(jnp.bfloat16)
    residual_wide = residual.astype(jnp.float32)
    feed_sq = first_sq + 2.0 * after_scale * cross_sum + after_scale * after_scale * branch_sq
    feed_scale = lax.rsqrt(feed_sq / D + epsilon)
    feed_input = (residual_wide * feed_scale[:, None] * gain_feed).astype(jnp.bfloat16)
    return (residual, feed_input)


def solution(mesh):
    in_specs = (
        P("tok", ("hx", "hy")),
        P(("hx", "hy")),
        P(("hx", "hy")),
        P(("hx", "hy")),
        P("tok", ("hx", "hy")),
        P("tok", ("hx", "hy")),
        P("tok", ("hx", "hy")),
        P(("hx", "hy"), "tok"),
        P("tok"),
    )
    out_specs = (P("tok", ("hx", "hy")), P("tok", ("hx", "hy")))
    return jax.shard_map(
        per_device, mesh=mesh, in_specs=in_specs, out_specs=out_specs, check_vma=False
    )
```

profile of v0, /device:TPU:8, one launch (start us, length us, event | category | flops | bytes accessed | tf_op | source)
XLA Modules:
  0.0 299.1 jit_solution(16729745893624223635)
XLA Ops:
  7.2 0.0 all-gather.6.cloned.1.call-start
  7.2 1.1 copy.42
  8.3 0.7 reshape.243
  9.0 0.7 maximum_bitcast_fusion
  9.7 0.0 all-gather.6.cloned.1.call-update
  9.7 0.0 all-gather.4.cloned.1.call-start
  9.7 1.6 pad_maximum_fusion
  11.3 0.0 all-gather.4.cloned.1.call-update
  11.4 2.5 broadcast_in_dim.63
  13.8 0.0 copy-start.1
  13.8 12.1 %all-to-all-start = ((bf16[32,256,144]{1,2,0:T(8,128)(2,1)}), bf16[32,256,144]{1,2,0:T(8,128)(2,1)S(1)}, u32[]{:S(2)}, u32[]{:S(2)}) async-start(bf16[32,256,144]{1,2,0:T(8,128)(2,1)} %broadcast_in_dim.63), calls=%async_computation | async-start | bytes 4718592 | tf_op jit(solution)/shard_map/all_to_all | solution.py:34
  25.9 0.0 reduce-scatter.2.cloned.1.call-start
  26.0 0.0 copy-done.1
  26.0 0.1 fusion.35
  26.1 0.5 multiply_cosine_fusion
  26.6 66.1 %all-gather.6.cloned.1.call-done = bf16[16,288,257]{1,2,0:T(8,128)(2,1)} async-done(((bf16[1,288,257]{1,2,0:T(8,128)(2,1)}), bf16[16,288,257]{1,2,0:T(8,128)(2,1)}) %all-gather.6.cloned.1.call-update) | async-done | bytes 2368528 | tf_op jit(solution)/shard_map/all_gather | solution.py:17
  92.7 4.1 %copy.43 = bf16[16,288,257]{1,0,2:T(8,128)(2,1)} copy(bf16[16,288,257]{1,2,0:T(8,128)(2,1)} %all-gather.6.cloned.1.call-done) | data formatting | bytes 4737024 | tf_op jit(solution)/shard_map/all_gather | solution.py:17
  96.8 6.2 %reshape.251 = bf16[4608,257]{0,1:T(8,128)(2,1)} reshape(bf16[16,288,257]{1,0,2:T(8,128)(2,1)} %copy.43) | data formatting | bytes 4737024
  103.0 0.9 fusion.51
  103.9 2.2 fusion
  106.2 58.8 %all-gather.4.cloned.1.call-done = bf16[4608,512]{1,0:T(8,128)(2,1)} async-done(((bf16[144,512]{1,0:T(8,128)(2,1)}), bf16[4608,512]{1,0:T(8,128)(2,1)}) %all-gather.4.cloned.1.call-update) | async-done | bytes 4718608 | tf_op jit(solution)/shard_map/all_gather | solution.py:28
  164.9 3.6 %fusion.3 = f32[256,256]{0,1:T(8,128)S(1)} fusion(bf16[4608,512]{1,0:T(8,128)(2,1)} %all-gather.4.cloned.1.call-done, f32[4608]{0:T(1024)S(1)} %fusion.51, f32[256]{0:T(256)S(1)} %add_rsqrt_fusion.2, bf16[4608,257]{0,1:T(8,128)(2,1)} %reshape.251), kind=kOutput, calls=%fused_computation.6 | convolution fusion | flops 608698368 | bytes 5000192 | tf_op jit(solution)/shard_map/dot_general | solution.py:100
  168.6 0.1 copy.56
  168.7 0.1 copy.57
  168.9 3.0 %fusion.9 = f32[256,1,128]{0,2,1:T(8,128)S(1)} fusion(bf16[4608,512]{1,0:T(8,128)(2,1)} %all-gather.4.cloned.1.call-done, f32[4608]{0:T(1024)S(1)} %fusion.51, f32[256]{0:T(256)S(1)} %add_rsqrt_fusion.2, bf16[4608,257]{0,1:T(8,128)(2,1)} %reshape.251), kind=kOutput, calls=%fused_computation.14 | convolution fusion | flops 306708480 | bytes 3689472 | tf_op jit(solution)/shard_map/dot_general | solution.py:100
  171.9 0.3 fusion.50
  172.2 0.1 multiply_subtract_fusion
  172.3 0.4 select_reduce_fusion
  172.7 0.1 fusion.22
  172.8 3.1 %fusion.19 = bf16[1,128,256,2]{2,1,3,0:T(8,128)(2,1)S(1)} fusion(bf16[4608,512]{1,0:T(8,128)(2,1)} %all-gather.4.cloned.1.call-done, f32[256,1,2,256]{0,3,2,1:T(8,128)S(1)} %get-tuple-element.36, f32[256,2]{0,1:T(2,128)S(1)} %get-tuple-element.35, pred[256,256]{0,1:T(8,128)(4,1)S(1)} %fusion.35, f32[256,2]{0,1:T(2,128)S(1)} %fusion.22, ...), kind=kOutput, calls=%fused_computation.18 | convolution fusion | flops 340819968 | bytes 4283392 | tf_op jit(solution)/shard_map/while/body/eval_jaxpr/tkrs,skh->tkrh/dot_general | solution.py:131
  175.9 0.0 all-to-all-done
  175.9 0.0 copy-start.2
  175.9 2.2 convolution_convert_fusion
  178.1 0.0 copy-start
  178.1 0.0 copy-start.3
  178.1 0.0 reduce-scatter.2.cloned.1.call-update
  178.1 0.0 copy-done.2
  178.1 94.7 %reduce-scatter.2.cloned.1.call-done = bf16[256,288]{0,1:T(8,128)(2,1)} async-done(((bf16[256,4608]{0,1:T(8,128)(2,1)}), bf16[256,288]{0,1:T(8,128)(2,1)}) %reduce-scatter.2.cloned.1.call-update) | async-done | bytes 147472 | tf_op jit(solution)/shard_map/reduce_scatter | solution.py:145
  272.8 0.0 copy-done
  272.8 1.0 fusion.26
  273.9 0.6 broadcast_in_dim.64
  274.5 6.3 %all-to-all-start.1 = ((f32[16,1,768]{2,1,0:T(1,128)}), f32[16,1,768]{2,1,0:T(1,128)S(1)}, u32[]{:S(2)}, u32[]{:S(2)}) async-start(f32[16,1,768]{2,1,0:T(1,128)} %broadcast_in_dim.64), calls=%async_computation.2 | async-start | bytes 98304 | tf_op jit(solution)/shard_map/all_to_all | solution.py:34
  280.8 0.0 copy-done.3
  280.8 10.0 %all-to-all-done.1 = f32[16,1,768]{2,1,0:T(1,128)S(1)} async-done(((f32[16,1,768]{2,1,0:T(1,128)}), f32[16,1,768]{2,1,0:T(1,128)S(1)}, u32[]{:S(2)}, u32[]{:S(2)}) %all-to-all-start.1) | async-done | bytes 49184 | tf_op jit(solution)/shard_map/all_to_all | solution.py:34
  290.9 1.8 multiply_convert_fusion
  (9 shorter events, 0.1 us)
Async XLA Ops:
  7.2 85.5 %all-gather.6.cloned.1.call-start = ((), (), s32[]{:S(2)}) async-start(), calls=%async_computation.5 | async-start | bytes 3446784 | tf_op jit(solution)/shard_map/all_gather | solution.py:17
  9.7 155.2 %all-gather.4.cloned.1.call-start = ((), (), s32[]{:S(2)}) async-start(), calls=%async_computation.3 | async-start | bytes 4866048 | tf_op jit(solution)/shard_map/all_gather | solution.py:28
  13.8 12.2 %copy-start.1 = (s32[256]{0:T(256)S(1)}, s32[256]{0:T(256)}, u32[]{:S(2)}) copy-start(s32[256]{0:T(256)} %param.17) | copy-start | bytes 3076
  13.8 162.0 %all-to-all-start = ((bf16[32,256,144]{1,2,0:T(8,128)(2,1)}), bf16[32,256,144]{1,2,0:T(8,128)(2,1)S(1)}, u32[]{:S(2)}, u32[]{:S(2)}) async-start(bf16[32,256,144]{1,2,0:T(8,128)(2,1)} %broadcast_in_dim.63), calls=%async_computation | async-start | bytes 4718592 | tf_op jit(solution)/shard_map/all_to_all | solution.py:34
  25.9 246.9 %reduce-scatter.2.cloned.1.call-start = ((), (), s32[]{:S(2)}) async-start(), calls=%async_computation.4 | async-start | bytes 2506752 | tf_op jit(solution)/shard_map/reduce_scatter | solution.py:145
  175.9 2.2 copy-start.2
  178.1 94.7 %copy-start = (bf16[256,288]{0,1:T(8,128)(2,1)S(1)}, bf16[256,288]{0,1:T(8,128)(2,1)}, u32[]{:S(2)}) copy-start(bf16[256,288]{0,1:T(8,128)(2,1)} %param.9) | copy-start | bytes 442372
  178.1 102.7 %copy-start.3 = (bf16[288]{0:T(512)(128)(2,1)S(1)}, bf16[288]{0:T(512)(128)(2,1)}, u32[]{:S(2)}) copy-start(bf16[288]{0:T(512)(128)(2,1)} %param.12) | copy-start | bytes 1732
  274.5 16.3 %all-to-all-start.1 = ((f32[16,1,768]{2,1,0:T(1,128)}), f32[16,1,768]{2,1,0:T(1,128)S(1)}, u32[]{:S(2)}, u32[]{:S(2)}) async-start(f32[16,1,768]{2,1,0:T(1,128)} %broadcast_in_dim.64), calls=%async_computation.2 | async-start | bytes 98304 | tf_op jit(solution)/shard_map/all_to_all | solution.py:34
Sparse Core Ops, SparseCore 0:
  11.0 81.6 all-gather.5
  95.4 69.4 all-gather.3
  178.2 94.5 reduce-scatter.1
where the time goes:
time: 300 us; the launch traced here: 299 us
  waiting for transfers between devices  230 us (77%)
  starting transfers between devices  18.5 us (6%)
  local copies, waits for them, and re-layouts  15.5 us (5%)
  between operations  13.9 us (5%)
  matrix products  12.3 us (4%)
  other arithmetic  9.49 us (3%)
    reduce_scatter x1, waiting for transfers between devices, per_device(): lax.psum_scatter(terms.astype(jnp.bfloat16), ('hx', 'hy'), scatter_dimens...  94.7 us
    all_gather x1, waiting for transfers between devices, rows_first(): lax.all_gather(both, axis, axis=0, tiled=True)  66.1 us
    all_gather x1, waiting for transfers between devices, side_by_side(): filled = lax.all_gather(both, axis, axis=dim, tiled=True)  58.8 us
    all_to_all x2, starting transfers between devices, copy_for_each(): return lax.all_to_all(copies, axis, split_axis=0, concat_axis=0, tiled=True)  18.3 us
    all_to_all x2, waiting for transfers between devices, copy_for_each(): return lax.all_to_all(copies, axis, split_axis=0, concat_axis=0, tiled=True)  10 us
    unnamed x12, local copies, waits for them, and re-layouts  7.58 us
    dot_general x2, matrix products, per_device(): jnp.dot(normed, piece, preferred_element_type=jnp.float32)  6.66 us
  transfers between devices with their start and end apart: 5, of which 4 were waited for; matrix products, arithmetic and copies ran while one was open for 10% of the time, Pallas kernels for 0%

commit v1 on v0

--- a/solution.py
+++ b/solution.py
@@ -11,10 +11,23 @@
 neg_big = -1e30
 
 
+def create_stocks(own_rows, a_name):
+    extra = jnp.concatenate(
+        lax.all_to_all(
+            jnp.stack([own_rows for _ in range(lax.axis_size(a_name))]),
+            axis_name=a_name,
+            split_axis=0,
+            concat_axis=0,
+        ),
+        axis=0,
+    )
+    return extra
+
+
 def rows_first(arrays, axis, dims):
     turned = [jnp.moveaxis(a, dim, 0) for a, dim in zip(arrays, dims)]
     both = jnp.concatenate([t.reshape(len(t), -1) for t in turned], axis=1)
-    filled, at, finished = (lax.all_gather(both, axis, axis=0, tiled=True), 0, [])
+    filled, at, finished = (create_stocks(both, axis), 0, [])
     for t, dim in zip(turned, dims):
         slab = filled[:, at : at + t[0].size].reshape(-1, *t.shape[1:])
         finished.append(jnp.moveaxis(slab, 0, dim))

time: 300 us -> 310 us (1.033)
  blocking collectives: 0 us -> 110 us
  waiting for transfers between devices: 230 us -> 130 us
    all_to_all x0 -> x1, blocking collectives: none -> 110 us  [create_stocks(): lax.all_to_all(jnp.stack([own_rows for _ in range(lax.axis_size(a_name))]...]
    all_gather x1 -> x0, waiting for transfers between devices: 66.1 us -> none  [rows_first(): lax.all_gather(both, axis, axis=0, tiled=True)]
    all_gather x1, waiting for transfers between devices: 58.8 us -> 0.02 us  [side_by_side(): filled = lax.all_gather(both, axis, axis=dim, tiled=True)]
    all_to_all x2, waiting for transfers between devices: 10 us -> 39.9 us  [copy_for_each(): return lax.all_to_all(copies, axis, split_axis=0, concat_axis=0, tiled=True)]
    unnamed x12, local copies, waits for them, and re-layouts: 7.58 us -> 0.27 us
    reshape x0 -> x1, local copies, waits for them, and re-layouts: none -> 6.24 us  [create_stocks(): jnp.concatenate(lax.all_to_all(jnp.stack([own_rows for _ in range(lax.axi...]
    reduce_scatter x1, waiting for transfers between devices: 94.7 us -> 90.6 us  [per_device(): lax.psum_scatter(terms.astype(jnp.bfloat16), ('hx', 'hy'), scatter_dimens...]
    all_to_all x0 -> x1, local copies, waits for them, and re-layouts: none -> 4.07 us  [create_stocks(): lax.all_to_all(jnp.stack([own_rows for _ in range(lax.axis_size(a_name))]...]
  transfers between devices with their start and end apart: 5 -> 4, of which waited for: 4 -> 3; matrix products, arithmetic and copies ran while one was open for 10% -> 9% of each run, Pallas kernels for 0% -> 0%
where the time goes in v1:
time: 310 us; the launch traced here: 309 us
  waiting for transfers between devices  130 us (42%)
  blocking collectives  110 us (35%)
  starting transfers between devices  18.4 us (6%)
  between operations  14.2 us (5%)
  local copies, waits for them, and re-layouts  14.1 us (5%)
  matrix products  12.3 us (4%)
  other arithmetic  9.73 us (3%)
    all_to_all x1, blocking collectives, create_stocks(): lax.all_to_all(jnp.stack([own_rows for _ in range(lax.axis_size(a_name))]...  110 us
    reduce_scatter x1, waiting for transfers between devices, per_device(): lax.psum_scatter(terms.astype(jnp.bfloat16), ('hx', 'hy'), scatter_dimens...  90.6 us
    all_to_all x2, waiting for transfers between devices, copy_for_each(): return lax.all_to_all(copies, axis, split_axis=0, concat_axis=0, tiled=True)  39.9 us
    all_to_all x2, starting transfers between devices, copy_for_each(): return lax.all_to_all(copies, axis, split_axis=0, concat_axis=0, tiled=True)  18.4 us
    dot_general x2, matrix products, per_device(): jnp.dot(normed, piece, preferred_element_type=jnp.float32)  6.66 us
    reshape x1, local copies, waits for them, and re-layouts, create_stocks(): jnp.concatenate(lax.all_to_all(jnp.stack([own_rows for _ in range(lax.axi...  6.24 us
  transfers between devices with their start and end apart: 4, of which 3 were waited for; matrix products, arithmetic and copies ran while one was open for 9% of the time, Pallas kernels for 0%

profile of v1, /device:TPU:8, one launch (start us, length us, event | category | flops | bytes accessed | tf_op | source)
XLA Modules:
  0.0 309.2 jit_solution(14369749622249803509)
XLA Ops:
  7.2 0.0 all-gather.2.cloned.1.call-start
  7.2 1.6 pad_maximum_fusion.1
  8.8 0.0 all-gather.2.cloned.1.call-update
  8.8 0.8 reshape.258
  9.6 0.9 pad_maximum_fusion
  10.6 0.2 copy.46
  10.7 0.3 stack.2
  11.0 0.0 copy-start.1
  11.0 110.0 %all_to_all.16 = bf16[16,288,257]{1,2,0:T(8,128)(2,1)} all-to-all(bf16[16,288,257]{1,2,0:T(8,128)(2,1)S(1)} %stack.2), channel_id=1, replica_groups=mesh['hx'=4,'hy'=4,'tok'=32] {'hx','hy'}, dimensions={0} | all-to-all | bytes 4737024 | tf_op jit(solution)/shard_map/all_to_all | solution.py:16
  121.0 0.0 copy-done.1
  121.0 1.6 broadcast_in_dim.63
  122.6 0.0 copy-start.2
  122.6 12.1 %all-to-all-start.1 = ((bf16[32,256,144]{1,2,0:T(8,128)(2,1)}), bf16[32,256,144]{1,2,0:T(8,128)(2,1)S(1)}, u32[]{:S(2)}, u32[]{:S(2)}) async-start(bf16[32,256,144]{1,2,0:T(8,128)(2,1)} %broadcast_in_dim.63), calls=%async_computation.1 | async-start | bytes 4718592 | tf_op jit(solution)/shard_map/all_to_all | solution.py:47
  134.7 0.0 reduce-scatter.2.cloned.1.call-start
  134.8 0.0 copy-done.2
  134.8 0.1 fusion.35
  134.9 0.5 multiply_cosine_fusion
  135.4 4.1 %copy.47 = bf16[16,288,257]{1,0,2:T(8,128)(2,1)} copy(bf16[16,288,257]{1,2,0:T(8,128)(2,1)} %all_to_all.16) | data formatting | bytes 4737024 | tf_op jit(solution)/shard_map/all_to_all | solution.py:16
  139.5 6.2 %reshape.249 = bf16[4608,257]{0,1:T(8,128)(2,1)} reshape(bf16[16,288,257]{1,0,2:T(8,128)(2,1)} %copy.47) | data formatting | bytes 4737024 | tf_op jit(solution)/shard_map/reshape | solution.py:15
  145.7 0.9 fusion.51
  146.7 2.2 fusion
  148.9 0.0 all-gather.2.cloned.1.call-done
  148.9 3.6 %fusion.3 = f32[256,256]{0,1:T(8,128)S(1)} fusion(bf16[4608,512]{1,0:T(8,128)(2,1)} %all-gather.2.cloned.1.call-done, f32[4608]{0:T(1024)S(1)} %fusion.51, f32[256]{0:T(256)S(1)} %add_rsqrt_fusion.2, bf16[4608,257]{0,1:T(8,128)(2,1)} %reshape.249), kind=kOutput, calls=%fused_computation.6 | convolution fusion | flops 608698368 | bytes 5000192 | tf_op jit(solution)/shard_map/dot_general | solution.py:113
  152.6 0.1 copy.60
  152.7 0.1 copy.61
  152.8 3.0 fusion.9
  155.9 0.3 fusion.50
  156.2 0.1 multiply_subtract_fusion
  156.3 0.4 select_reduce_fusion
  156.6 0.1 fusion.22
  156.8 3.1 fusion.19
  159.8 29.9 %all-to-all-done.1 = bf16[32,256,144]{1,2,0:T(8,128)(2,1)S(1)} async-done(((bf16[32,256,144]{1,2,0:T(8,128)(2,1)}), bf16[32,256,144]{1,2,0:T(8,128)(2,1)S(1)}, u32[]{:S(2)}, u32[]{:S(2)}) %all-to-all-start.1) | async-done | bytes 2359328 | tf_op jit(solution)/shard_map/all_to_all | solution.py:47
  189.7 0.0 copy-start.3
  189.7 2.2 convolution_convert_fusion
  191.9 0.0 copy-start
  191.9 0.0 copy-start.4
  191.9 0.0 reduce-scatter.2.cloned.1.call-update
  191.9 0.0 copy-done.3
  191.9 90.6 %reduce-scatter.2.cloned.1.call-done = bf16[256,288]{0,1:T(8,128)(2,1)} async-done(((bf16[256,4608]{0,1:T(8,128)(2,1)}), bf16[256,288]{0,1:T(8,128)(2,1)}) %reduce-scatter.2.cloned.1.call-update) | async-done | bytes 147472 | tf_op jit(solution)/shard_map/reduce_scatter | solution.py:158
  282.5 0.0 copy-done
  282.5 1.0 fusion.26
  283.6 0.6 broadcast_in_dim.64
  284.2 6.3 %all-to-all-start.2 = ((f32[16,1,768]{2,1,0:T(1,128)}), f32[16,1,768]{2,1,0:T(1,128)S(1)}, u32[]{:S(2)}, u32[]{:S(2)}) async-start(f32[16,1,768]{2,1,0:T(1,128)} %broadcast_in_dim.64), calls=%async_computation.3 | async-start | bytes 98304 | tf_op jit(solution)/shard_map/all_to_all | solution.py:47
  290.5 0.0 copy-done.4
  290.5 10.0 %all-to-all-done.2 = f32[16,1,768]{2,1,0:T(1,128)S(1)} async-done(((f32[16,1,768]{2,1,0:T(1,128)}), f32[16,1,768]{2,1,0:T(1,128)S(1)}, u32[]{:S(2)}, u32[]{:S(2)}) %all-to-all-start.2) | async-done | bytes 49184 | tf_op jit(solution)/shard_map/all_to_all | solution.py:47
  300.6 1.8 multiply_convert_fusion
  (9 shorter events, 0.1 us)
Async XLA Ops:
  7.2 141.7 %all-gather.2.cloned.1.call-start = ((), (), s32[]{:S(2)}) async-start(), calls=%async_computation.4 | async-start | bytes 4866048 | tf_op jit(solution)/shard_map/all_gather | solution.py:41
  11.0 110.0 %copy-start.1 = (bf16[256,144]{0,1:T(8,128)(2,1)S(1)}, bf16[256,144]{0,1:T(8,128)(2,1)}, u32[]{:S(2)}) copy-start(bf16[256,144]{0,1:T(8,128)(2,1)} %param.16) | copy-start | bytes 221188
  122.6 12.2 %copy-start.2 = (s32[256]{0:T(256)S(1)}, s32[256]{0:T(256)}, u32[]{:S(2)}) copy-start(s32[256]{0:T(256)} %param.17) | copy-start | bytes 3076
  122.6 67.1 %all-to-all-start.1 = ((bf16[32,256,144]{1,2,0:T(8,128)(2,1)}), bf16[32,256,144]{1,2,0:T(8,128)(2,1)S(1)}, u32[]{:S(2)}, u32[]{:S(2)}) async-start(bf16[32,256,144]{1,2,0:T(8,128)(2,1)} %broadcast_in_dim.63), calls=%async_computation.1 | async-start | bytes 4718592 | tf_op jit(solution)/shard_map/all_to_all | solution.py:47
  134.7 147.8 %reduce-scatter.2.cloned.1.call-start = ((), (), s32[]{:S(2)}) async-start(), calls=%async_computation.5 | async-start | bytes 2506752 | tf_op jit(solution)/shard_map/reduce_scatter | solution.py:158
  189.7 2.2 copy-start.3
  191.9 90.6 %copy-start = (bf16[256,288]{0,1:T(8,128)(2,1)S(1)}, bf16[256,288]{0,1:T(8,128)(2,1)}, u32[]{:S(2)}) copy-start(bf16[256,288]{0,1:T(8,128)(2,1)} %param.9) | copy-start | bytes 442372
  191.9 98.6 %copy-start.4 = (bf16[288]{0:T(512)(128)(2,1)S(1)}, bf16[288]{0:T(512)(128)(2,1)}, u32[]{:S(2)}) copy-start(bf16[288]{0:T(512)(128)(2,1)} %param.12) | copy-start | bytes 1732
  284.2 16.3 %all-to-all-start.2 = ((f32[16,1,768]{2,1,0:T(1,128)}), f32[16,1,768]{2,1,0:T(1,128)S(1)}, u32[]{:S(2)}, u32[]{:S(2)}) async-start(f32[16,1,768]{2,1,0:T(1,128)} %broadcast_in_dim.64), calls=%async_computation.3 | async-start | bytes 98304 | tf_op jit(solution)/shard_map/all_to_all | solution.py:47
Sparse Core Ops, SparseCore 0:
  10.7 97.2 all-gather.1
  192.0 90.4 reduce-scatter.1
